TPU v7x, 32 devices: a 4x4x1 block of a 4x4x8 slice. The times are simulated.
32 devices in a mesh: rep: 2 (over z, core), dp: 16 (over x, y).
Axes of the slice: x: 4, y: 4, z: 1, core: 2. Of those that a mesh axis runs over, the one named last changes fastest.
The devices are a block of a 4x4x8 slice.
Arguments:
- a: bfloat16 [32, 4, 4096, 512], P(('rep', 'dp')), parts along dimension 0
- g: bfloat16 [32, 4, 4096, 1664], P(('rep', 'dp')), parts along dimension 0
Outputs:
- output: bfloat16 [8, 512, 1664], P('rep'), parts along dimension 0
There are 2 independent parts. A program takes and returns all parts, laid end to end along the dimension named above; each array names one.
All inputs are finite; a program needn't handle non-finite values.
Results may differ from a plain program's by a relative error of at most 0.012.
Values are sent between devices in bfloat16 or wider.
A program may use at most 768 MiB of HBM per device.

v0:
```python
import jax
import jax.numpy as jnp


def solution(mesh):
    groups = mesh.shape["rep"]

    def step(a, g):
        a, g = (t.reshape(groups, -1, *t.shape[1:]) for t in (a, g))
        sums = jnp.einsum("rsntd,rsntf->rndf", a, g, preferred_element_type=jnp.float32)
        return sums.astype(jnp.bfloat16).reshape(-1, *sums.shape[2:])

    return step
```

profile of v0, /device:TPU:96, one launch (start us, length us, event | category | flops | bytes accessed | tf_op | source)
XLA Modules:
  0.0 339.4 jit_solution(10862160661217155946)
XLA Ops:
  0.0 39.5 %fusion.3 = f32[1,4,512,1664]{3,2,1,0:T(8,128)} fusion(bf16[1,4,4096,1664]{3,2,1,0:T(8,128)(2,1)} %param.1, bf16[1,4,4096,512]{3,2,1,0:T(8,128)(2,1)} %param), kind=kOutput, calls=%fused_computation.4 | convolution fusion | flops 27917287424 | bytes 84934656 | tf_op jit(solution)/rsntd,rsntf->rndf/dot_general | solution.py:10
  39.5 299.8 %all-reduce.2 = bf16[1,4,512,1664]{3,2,1,0:T(8,128)(2,1)} all-reduce(f32[1,4,512,1664]{3,2,1,0:T(8,128)} %fusion.3), channel_id=1, replica_groups=[2,16]<=[32], use_global_device_ids=true, to_apply=%add.clone | all-reduce | flops 3407872 | bytes 20447232 | tf_op jit(solution)/rsntd,rsntf->rndf/dot_general | solution.py:10
where the time goes:
time: 339 us
  blocking collectives  300 us (88%)
  matrix products  39.5 us (12%)
    dot_general x1, blocking collectives, step(): jnp.einsum('rsntd,rsntf->rndf', a, g, preferred_element_type=jnp.float32)  300 us
    dot_general x1, matrix products, step(): jnp.einsum('rsntd,rsntf->rndf', a, g, preferred_element_type=jnp.float32)  39.5 us

commit v1 on v0

v1 whole, which is shorter than its diff:
```python
import functools

import jax
import jax.numpy as jnp
from jax import lax
from jax.experimental import pallas as pl
from jax.experimental.pallas import tpu as pltpu
from jax.sharding import PartitionSpec as P

MESH = pl.DeviceIdType.MESH
SIDE = 4
LANES = 128
TILES = (4, 4, 5)
LAG = (0, 2, 4, 6, 8, 10, 12, 14, 16)
K_PARTS = 2


def kernel(a_hbm, g_hbm, o_hbm, a_buf, g_buf, terms, s0, r1, s1, r2, rows, s2, r3, s3, r4, out,
           a_sem, g_sem, send_sem, recv_sem, out_sem):
    count, tokens, d_model = a_hbm.shape
    columns = []
    for t in TILES:
        columns.append((sum(w for _, w in columns), t * LANES))
    per = len(columns)
    half_rows = d_model // 2
    block = half_rows // SIDE
    side_rows = block // 2
    sub = block // SIDE
    part = tokens // K_PARTS

    me = lax.axis_index("dp")
    px, py = me // SIDE, me % SIDE

    def wrap(p):
        return (p + 2 * SIDE) % SIDE

    first = (px, py)
    second = (py, px)

    def at_first(h, p):
        return {"dp": wrap(p) * SIDE + py if h == 0 else px * SIDE + wrap(p)}

    def at_second(h, p):
        return {"dp": px * SIDE + wrap(p) if h == 0 else wrap(p) * SIDE + py}

    def of(h, p, q=0):
        return pl.multiple_of(h * half_rows + wrap(p) * block + wrap(q) * sub, sub)

    def a_load(n, k):
        slot = n % 2
        return pltpu.make_async_copy(
            a_hbm.at[n, pl.ds(k * part, part)], a_buf.at[slot, pl.ds(k * part, part)], a_sem.at[slot, k])

    def g_load(n, j, k):
        c, w = columns[j]
        slot = (n * per + j) % 2
        return pltpu.make_async_copy(
            g_hbm.at[n, pl.ds(k * part, part), pl.ds(c, w)],
            g_buf.at[slot, pl.ds(k * part, part), pl.ds(0, w)], g_sem.at[slot, k])

    for k in range(K_PARTS):
        a_load(0, k).start()
        g_load(0, 0, k).start()

    barrier = pltpu.get_barrier_semaphore()
    for d in (1, -1):
        pl.semaphore_signal(barrier, inc=1, device_id=at_first(0, px + d), device_id_type=MESH)
        pl.semaphore_signal(barrier, inc=1, device_id=at_second(0, py + d), device_id_type=MESH)

    pl.semaphore_wait(barrier, SIDE)

    def matmul(n, j):
        c, w = columns[j]
        slot, a_slot = (n * per + j) % 2, n % 2
        if j == 0:
            @pl.when(n + 1 < count)
            def _():
                for k in range(K_PARTS):
                    a_load(n + 1, k).start()
        if j + 1 < per:
            for k in range(K_PARTS):
                g_load(n, j + 1, k).start()
        else:
            @pl.when(n + 1 < count)
            def _():
                for k in range(K_PARTS):
                    g_load(n + 1, 0, k).start()

        for k in range(K_PARTS):
            if j == 0:
                a_load(n, k).wait()
            g_load(n, j, k).wait()

        def over(k, _):
            k0 = pl.multiple_of(k * part, part)
            term = lax.dot_general(
                a_buf[a_slot, pl.ds(k0, part), :], g_buf[slot, pl.ds(k0, part), pl.ds(0, w)],
                (((0,), (0,)), ((), ())), preferred_element_type=jnp.float32)

            @pl.when(k == 0)
            def _():
                terms[n, :, pl.ds(c, w)] = term

            @pl.when(k > 0)
            def _():
                terms[n, :, pl.ds(c, w)] += term
            return 0

        lax.fori_loop(0, K_PARTS, over, 0)

    def stages(n, j):
        c, w = columns[j]
        cols = pl.ds(c, w)
        unit = n * per + j

        def term(row, size):
            return terms[n, pl.ds(row, size), cols]

        def send(h, src, dst, kind, device):
            pltpu.make_async_remote_copy(
                src_ref=src, dst_ref=dst, send_sem=send_sem.at[2 * unit + h], recv_sem=recv_sem.at[kind, 2 * unit + h],
                device_id=device, device_id_type=MESH).start()

        def arrived(h, kind, size):
            ref = out.at[n, pl.ds(0, size), cols]
            pltpu.make_async_copy(ref, ref, recv_sem.at[kind, 2 * unit + h]).wait()

        def at(buf, h, i, size):
            return buf.at[n, h, pl.ds(i * size, size), cols]

        def place(row, size):
            return out.at[n, pl.ds(row, size), cols]

        def turn(h):
            return 1 - 2 * ((unit + h) % 2)

        half = side_rows

        def stage0():
            for h in (0, 1):
                p = first[h]
                s0[n, h, pl.ds(0, block), cols] = term(of(h, p + 2), block).astype(jnp.bfloat16)
                s0[n, h, pl.ds(2 * half, half), cols] = term(of(h, p - 1) + half, half).astype(jnp.bfloat16)
                s0[n, h, pl.ds(3 * half, half), cols] = term(of(h, p + 1), half).astype(jnp.bfloat16)
                send(h, at(s0, h, 0, half), at(r1, h, 0, half), 0, at_first(h, p - 1))
                send(h, at(s0, h, 1, half), at(r1, h, 1, half), 0, at_first(h, p + 1))
                send(h, at(s0, h, 2, half), at(r2, h, 3, half), 1, at_first(h, p - 1))
                send(h, at(s0, h, 3, half), at(r2, h, 2, half), 1, at_first(h, p + 1))

        def stage1():
            for h in (0, 1):
                p = first[h]
                arrived(h, 0, 2 * half)
                got = r1[n, h, :, cols].astype(jnp.float32)
                s1[n, h, pl.ds(0, half), cols] = (got[:half] + term(of(h, p - 1), half)).astype(jnp.bfloat16)
                s1[n, h, pl.ds(half, half), cols] = (got[half:] + term(of(h, p + 1) + half, half)).astype(jnp.bfloat16)
                send(h, at(s1, h, 0, half), at(r2, h, 0, half), 1, at_first(h, p - 1))
                send(h, at(s1, h, 1, half), at(r2, h, 1, half), 1, at_first(h, p + 1))

        def stage2():
            for h in (0, 1):
                p, q, t = first[h], second[h], turn(h)
                arrived(h, 1, 4 * half)
                got = r2[n, h, :, cols].astype(jnp.float32)
                rows[n, h, :, cols] = got[:block] + got[block:] + term(of(h, p), block)

                def mine(i):
                    return rows[n, h, pl.ds(pl.multiple_of(wrap(i) * sub, sub), sub), cols].astype(jnp.bfloat16)

                s2[n, h, pl.ds(0, sub), cols] = mine(q + 2)
                s2[n, h, pl.ds(sub, sub), cols] = mine(q + t)
                send(h, at(s2, h, 0, sub), at(r3, h, 0, sub), 2, at_second(h, q - t))
                send(h, at(s2, h, 1, sub), at(r4, h, 1, sub), 3, at_second(h, q + t))

        def stage3():
            for h in (0, 1):
                q, t = second[h], turn(h)
                arrived(h, 2, sub)
                got = r3[n, h, :, cols].astype(jnp.float32)
                s3[n, h, :, cols] = (
                    got + rows[n, h, pl.ds(pl.multiple_of(wrap(q - t) * sub, sub), sub), cols]).astype(jnp.bfloat16)
                send(h, at(s3, h, 0, sub), at(r4, h, 0, sub), 3, at_second(h, q - t))

        def stage4():
            for h in (0, 1):
                p, q = first[h], second[h]
                arrived(h, 3, 2 * sub)
                got = r4[n, h, :, cols].astype(jnp.float32)
                total = got[:sub] + got[sub:] + rows[n, h, pl.ds(pl.multiple_of(q * sub, sub), sub), cols]
                row = of(h, p, q)
                out[n, pl.ds(row, sub), cols] = total.astype(jnp.bfloat16)
                for d in (1, -1):
                    send(h, place(row, sub), place(row, sub), 4, at_second(h, q + d))

        def stage5():
            for h in (0, 1):
                p, q, t = first[h], second[h], turn(h)
                arrived(h, 4, 2 * sub)
                row = of(h, p, q - t)
                send(h, place(row, sub), place(row, sub), 5, at_second(h, q + t))

        def stage6():
            for h in (0, 1):
                p = first[h]
                arrived(h, 5, sub)
                row = of(h, p)
                for d in (1, -1):
                    send(h, place(row, block), place(row, block), 6, at_first(h, p + d))

        def stage7():
            for h in (0, 1):
                p = first[h]
                arrived(h, 6, 2 * block)
                row = of(h, p - 1)
                send(h, place(row, half), place(row, half), 7, at_first(h, p + 1))
                row = of(h, p + 1) + half
                send(h, place(row, half), place(row, half), 7, at_first(h, p - 1))

        def stage8():
            for h in (0, 1):
                arrived(h, 7, 2 * half)
            pltpu.make_async_copy(out.at[n, :, cols], o_hbm.at[n, :, cols], out_sem.at[unit]).start()

        return stage0, stage1, stage2, stage3, stage4, stage5, stage6, stage7, stage8

    def step(it, _):
        for j in range(per):
            for s in range(len(LAG) - 1, 0, -1):
                back = (LAG[s] - j + per - 1) // per
                jj = (j - LAG[s]) % per
                n = it - back

                @pl.when((n >= 0) & (n < count))
                def _():
                    stages(n, jj)[s]()

            @pl.when(it < count)
            def _():
                matmul(it, j)
                stages(it, j)[0]()
        return 0

    lax.fori_loop(0, count + -(-LAG[-1] // per), step, 0)

    sent = 15 * half_rows // 8
    def finish(n, _):
        for j, (c, w) in enumerate(columns):
            unit = n * per + j
            for h in (0, 1):
                ref = out.at[n, pl.ds(0, sent), pl.ds(c, w)]
                pltpu.make_async_copy(ref, ref, send_sem.at[2 * unit + h]).wait()
            pltpu.make_async_copy(out.at[n, :, pl.ds(c, w)], o_hbm.at[n, :, pl.ds(c, w)], out_sem.at[unit]).wait()
        return 0

    lax.fori_loop(0, count, finish, 0)


def solution(mesh):
    def step(a, g):
        a, g = a.reshape(a.shape[1:]), g.reshape(g.shape[1:])
        count, tokens, d_model = a.shape
        ff = g.shape[2]
        assert mesh.shape["dp"] == SIDE * SIDE and sum(TILES) * LANES == ff
        units = count * len(TILES)
        bf16, f32 = jnp.bfloat16, jnp.float32
        half_rows = d_model // 2
        block = half_rows // SIDE
        sub = block // SIDE
        VMEM, DMA = pltpu.VMEM, pltpu.SemaphoreType.DMA
        return pl.pallas_call(
            kernel,
            out_shape=jax.ShapeDtypeStruct((count, d_model, ff), bf16),
            in_specs=[pl.BlockSpec(memory_space=pl.ANY)] * 2,
            out_specs=pl.BlockSpec(memory_space=pl.ANY),
            scratch_shapes=[
                VMEM((2, tokens, d_model), bf16),
                VMEM((2, tokens, max(TILES) * LANES), bf16),
                VMEM((count, d_model, ff), f32),
                VMEM((count, 2, 2 * block, ff), bf16),
                VMEM((count, 2, block, ff), bf16),
                VMEM((count, 2, block, ff), bf16),
                VMEM((count, 2, 2 * block, ff), bf16),
                VMEM((count, 2, block, ff), f32),
                VMEM((count, 2, 2 * sub, ff), bf16),
                VMEM((count, 2, sub, ff), bf16),
                VMEM((count, 2, sub, ff), bf16),
                VMEM((count, 2, 2 * sub, ff), bf16),
                VMEM((count, d_model, ff), bf16),
                DMA((2, K_PARTS)),
                DMA((2, K_PARTS)),
                DMA((2 * units,)),
                DMA((8, 2 * units)),
                DMA((units,)),
            ],
            compiler_params=pltpu.CompilerParams(
                collective_id=0, has_side_effects=True, vmem_limit_bytes=67043328),
            name="sums",
        )(a, g)

    return jax.shard_map(
        step, mesh=mesh, in_specs=(P(("rep", "dp")), P(("rep", "dp"))), out_specs=P("rep"), check_vma=False)
```

time: 339 us -> 105 us (0.31)
  blocking collectives: 300 us -> 0 us
  Pallas kernels: 0 us -> 98.1 us
  matrix products: 39.5 us -> 0 us
  local copies, waits for them, and re-layouts: 0 us -> 6.31 us
    dot_general x1 -> x0, blocking collectives: 300 us -> none  [step(): jnp.einsum('rsntd,rsntf->rndf', a, g, preferred_element_type=jnp.float32)]
    pallas_call x0 -> x1, Pallas kernels: none -> 98.1 us  [step(): pl.pallas_call(kernel, out_shape=jax.ShapeDtypeStruct((count, d_model, ff...]
    dot_general x1 -> x0, matrix products: 39.5 us -> none  [step(): jnp.einsum('rsntd,rsntf->rndf', a, g, preferred_element_type=jnp.float32)]
    unnamed x0 -> x1, local copies, waits for them, and re-layouts: none -> 6.31 us
where the time goes in v1:
time: 105 us; the launch traced here: 104 us
  Pallas kernels  98.1 us (93%)
  local copies, waits for them, and re-layouts  6.31 us (6%)
    pallas_call x1, Pallas kernels, step(): pl.pallas_call(kernel, out_shape=jax.ShapeDtypeStruct((count, d_model, ff...  98.1 us
    unnamed x1, local copies, waits for them, and re-layouts  6.31 us

profile of v1, /device:TPU:96, one launch (start us, length us, event | category | flops | bytes accessed | tf_op | source)
XLA Modules:
  0.0 104.4 jit_solution(14573219478421065276)
XLA Ops:
  0.0 98.1 %sums.1 = bf16[4,512,1664]{2,1,0:T(8,128)(2,1)} custom-call(bf16[4,4096,512]{2,1,0:T(8,128)(2,1)} %bitcast.3, bf16[4,4096,1664]{2,1,0:T(8,128)(2,1)} %bitcast.2), custom_call_target="tpu_custom_call" | custom-call | tf_op jit(solution)/shard_map/sums/pallas_call | solution.py:270
  98.1 6.3 %copy.4 = bf16[4,512,1664]{2,1,0:T(8,128)(2,1)} copy(bf16[4,512,1664]{2,1,0:T(8,128)(2,1)} %sums.1) | data formatting | bytes 13631488

commit v2 on v1

v2 whole, which is shorter than its diff:
```python
import functools

import jax
import jax.numpy as jnp
from jax import lax
from jax.experimental import pallas as pl
from jax.experimental.pallas import tpu as pltpu
from jax.sharding import PartitionSpec as P

MESH = pl.DeviceIdType.MESH
SIDE = 4
LANES = 128
TILES = (7, 6)
LAG = (0, 3, 6, 9, 12, 15, 18, 21, 24)


def kernel(a_hbm, g_hbm, out, a_buf, g_buf, terms, s0, r1, s1, r2, rows, s2, r3, s3, r4,
           a_sem, g_sem, send_sem, recv_sem):
    count, tokens, d_model = a_hbm.shape
    columns = []
    for t in TILES:
        columns.append((sum(w for _, w in columns), t * LANES))
    per = len(columns)
    half_rows = d_model // 2
    block = half_rows // SIDE
    side_rows = block // 2
    sub = block // SIDE

    me = lax.axis_index("dp")
    px, py = me // SIDE, me % SIDE

    def wrap(p):
        return (p + 2 * SIDE) % SIDE

    first = (px, py)
    second = (py, px)

    def at_first(h, p):
        return {"dp": wrap(p) * SIDE + py if h == 0 else px * SIDE + wrap(p)}

    def at_second(h, p):
        return {"dp": px * SIDE + wrap(p) if h == 0 else wrap(p) * SIDE + py}

    def of(h, p, q=0):
        return pl.multiple_of(h * half_rows + wrap(p) * block + wrap(q) * sub, sub)

    def a_load(n, h):
        rows_of = pl.ds(h * half_rows, half_rows)
        return pltpu.make_async_copy(a_hbm.at[n, :, rows_of], a_buf.at[n % 2, :, rows_of], a_sem.at[n % 2, h])

    def g_load(n, j):
        c, w = columns[j]
        slot = (n * per + j) % 2
        return pltpu.make_async_copy(g_hbm.at[n, :, pl.ds(c, w)], g_buf.at[slot, :, pl.ds(0, w)], g_sem.at[slot])

    a_load(0, 0).start()
    g_load(0, 0).start()
    a_load(0, 1).start()

    barrier = pltpu.get_barrier_semaphore()
    for d in (1, -1):
        pl.semaphore_signal(barrier, inc=1, device_id=at_first(0, px + d), device_id_type=MESH)
        pl.semaphore_signal(barrier, inc=1, device_id=at_second(0, py + d), device_id_type=MESH)

    pl.semaphore_wait(barrier, SIDE)

    def matmul(n, j, h):
        c, w = columns[j]
        if j == 0:
            a_load(n, h).wait()

            @pl.when(n + 1 < count)
            def _():
                a_load(n + 1, h).start()
        if h == 0:
            g_load(n, j).wait()
            if j + 1 < per:
                g_load(n, j + 1).start()
            else:
                @pl.when(n + 1 < count)
                def _():
                    g_load(n + 1, 0).start()
        mine = pl.ds(h * half_rows, half_rows)
        terms[n, mine, pl.ds(c, w)] = lax.dot_general(
            a_buf[n % 2, :, mine], g_buf[(n * per + j) % 2, :, pl.ds(0, w)],
            (((0,), (0,)), ((), ())), preferred_element_type=jnp.float32)

    def stages(n, j, h):
        c, w = columns[j]
        cols = pl.ds(c, w)
        unit = n * per + j

        def term(row, size):
            return terms[n, pl.ds(row, size), cols]

        def send(h, src, dst, kind, device):
            pltpu.make_async_remote_copy(
                src_ref=src, dst_ref=dst, send_sem=send_sem.at[2 * unit + h], recv_sem=recv_sem.at[kind, 2 * unit + h],
                device_id=device, device_id_type=MESH).start()

        def arrived(h, kind, size):
            ref = out.at[n, pl.ds(0, size), cols]
            pltpu.make_async_copy(ref, ref, recv_sem.at[kind, 2 * unit + h]).wait()

        def at(buf, h, i, size):
            return buf.at[n, h, pl.ds(i * size, size), cols]

        def place(row, size):
            return out.at[n, pl.ds(row, size), cols]

        def turn(h):
            return 1 - 2 * ((unit + h) % 2)

        half = side_rows

        def stage0():
            p = first[h]
            s0[n, h, pl.ds(0, block), cols] = term(of(h, p + 2), block).astype(jnp.bfloat16)
            s0[n, h, pl.ds(2 * half, half), cols] = term(of(h, p - 1) + half, half).astype(jnp.bfloat16)
            s0[n, h, pl.ds(3 * half, half), cols] = term(of(h, p + 1), half).astype(jnp.bfloat16)
            send(h, at(s0, h, 0, half), at(r1, h, 0, half), 0, at_first(h, p - 1))
            send(h, at(s0, h, 1, half), at(r1, h, 1, half), 0, at_first(h, p + 1))
            send(h, at(s0, h, 2, half), at(r2, h, 3, half), 1, at_first(h, p - 1))
            send(h, at(s0, h, 3, half), at(r2, h, 2, half), 1, at_first(h, p + 1))

        def stage1():
            p = first[h]
            arrived(h, 0, 2 * half)
            got = r1[n, h, :, cols].astype(jnp.float32)
            s1[n, h, pl.ds(0, half), cols] = (got[:half] + term(of(h, p - 1), half)).astype(jnp.bfloat16)
            s1[n, h, pl.ds(half, half), cols] = (got[half:] + term(of(h, p + 1) + half, half)).astype(jnp.bfloat16)
            send(h, at(s1, h, 0, half), at(r2, h, 0, half), 1, at_first(h, p - 1))
            send(h, at(s1, h, 1, half), at(r2, h, 1, half), 1, at_first(h, p + 1))

        def stage2():
            p, q, t = first[h], second[h], turn(h)
            arrived(h, 1, 4 * half)
            got = r2[n, h, :, cols].astype(jnp.float32)
            rows[n, h, :, cols] = got[:block] + got[block:] + term(of(h, p), block)

            def mine(i):
                return rows[n, h, pl.ds(pl.multiple_of(wrap(i) * sub, sub), sub), cols].astype(jnp.bfloat16)

            s2[n, h, pl.ds(0, sub), cols] = mine(q + 2)
            s2[n, h, pl.ds(sub, sub), cols] = mine(q + t)
            send(h, at(s2, h, 0, sub), at(r3, h, 0, sub), 2, at_second(h, q - t))
            send(h, at(s2, h, 1, sub), at(r4, h, 1, sub), 3, at_second(h, q + t))

        def stage3():
            q, t = second[h], turn(h)
            arrived(h, 2, sub)
            got = r3[n, h, :, cols].astype(jnp.float32)
            s3[n, h, :, cols] = (
                got + rows[n, h, pl.ds(pl.multiple_of(wrap(q - t) * sub, sub), sub), cols]).astype(jnp.bfloat16)
            send(h, at(s3, h, 0, sub), at(r4, h, 0, sub), 3, at_second(h, q - t))

        def stage4():
            p, q = first[h], second[h]
            arrived(h, 3, 2 * sub)
            got = r4[n, h, :, cols].astype(jnp.float32)
            total = got[:sub] + got[sub:] + rows[n, h, pl.ds(pl.multiple_of(q * sub, sub), sub), cols]
            row = of(h, p, q)
            out[n, pl.ds(row, sub), cols] = total.astype(jnp.bfloat16)
            for d in (1, -1):
                send(h, place(row, sub), place(row, sub), 4, at_second(h, q + d))

        def stage5():
            p, q, t = first[h], second[h], turn(h)
            arrived(h, 4, 2 * sub)
            row = of(h, p, q - t)
            send(h, place(row, sub), place(row, sub), 5, at_second(h, q + t))

        def stage6():
            p = first[h]
            arrived(h, 5, sub)
            row = of(h, p)
            for d in (1, -1):
                send(h, place(row, block), place(row, block), 6, at_first(h, p + d))

        def stage7():
            p = first[h]
            arrived(h, 6, 2 * block)
            row = of(h, p - 1)
            send(h, place(row, half), place(row, half), 7, at_first(h, p + 1))
            row = of(h, p + 1) + half
            send(h, place(row, half), place(row, half), 7, at_first(h, p - 1))

        def stage8():
            arrived(h, 7, 2 * half)

        return stage0, stage1, stage2, stage3, stage4, stage5, stage6, stage7, stage8

    def step(it, _):
        for tick in range(2 * per):
            for s in range(len(LAG) - 1, 0, -1):
                back = -((tick - LAG[s]) // (2 * per))
                then = (tick - LAG[s]) % (2 * per)
                n = it - back

                @pl.when((n >= 0) & (n < count))
                def _():
                    stages(n, then // 2, then % 2)[s]()

            @pl.when(it < count)
            def _():
                matmul(it, tick // 2, tick % 2)
                stages(it, tick // 2, tick % 2)[0]()
        return 0

    lax.fori_loop(0, count + -(-LAG[-1] // (2 * per)), step, 0)

    sent = 15 * half_rows // 8
    def finish(n, _):
        for j, (c, w) in enumerate(columns):
            unit = n * per + j
            for h in (0, 1):
                ref = out.at[n, pl.ds(0, sent), pl.ds(c, w)]
                pltpu.make_async_copy(ref, ref, send_sem.at[2 * unit + h]).wait()
        return 0

    lax.fori_loop(0, count, finish, 0)


def solution(mesh):
    def step(a, g):
        a, g = a.reshape(a.shape[1:]), g.reshape(g.shape[1:])
        count, tokens, d_model = a.shape
        ff = g.shape[2]
        assert mesh.shape["dp"] == SIDE * SIDE and sum(TILES) * LANES == ff
        units = count * len(TILES)
        bf16, f32 = jnp.bfloat16, jnp.float32
        half_rows = d_model // 2
        block = half_rows // SIDE
        sub = block // SIDE
        VMEM, DMA = pltpu.VMEM, pltpu.SemaphoreType.DMA
        return pl.pallas_call(
            kernel,
            out_shape=VMEM((count, d_model, ff), bf16),
            in_specs=[pl.BlockSpec(memory_space=pl.ANY)] * 2,
            out_specs=pl.BlockSpec(memory_space=VMEM),
            scratch_shapes=[
                VMEM((2, tokens, d_model), bf16),
                VMEM((2, tokens, max(TILES) * LANES), bf16),
                VMEM((count, d_model, ff), f32),
                VMEM((count, 2, 2 * block, ff), bf16),
                VMEM((count, 2, block, ff), bf16),
                VMEM((count, 2, block, ff), bf16),
                VMEM((count, 2, 2 * block, ff), bf16),
                VMEM((count, 2, block, ff), f32),
                VMEM((count, 2, 2 * sub, ff), bf16),
                VMEM((count, 2, sub, ff), bf16),
                VMEM((count, 2, sub, ff), bf16),
                VMEM((count, 2, 2 * sub, ff), bf16),
                DMA((2, 2)),
                DMA((2,)),
                DMA((2 * units,)),
                DMA((8, 2 * units)),
            ],
            compiler_params=pltpu.CompilerParams(
                collective_id=0, has_side_effects=True, vmem_limit_bytes=57 * 1024 * 1024),
            name="sums",
        )(a, g)

    return jax.shard_map(
        step, mesh=mesh, in_specs=(P(("rep", "dp")), P(("rep", "dp"))), out_specs=P("rep"), check_vma=False)
```

time: 105 us -> 95.1 us (0.906)
  Pallas kernels: 98.1 us -> 92.1 us
  local copies, waits for them, and re-layouts: 6.31 us -> 2.88 us
    pallas_call x1, Pallas kernels: 98.1 us -> 92.1 us  [step(): pl.pallas_call(kernel, out_shape=VMEM((count, d_model, ff), bf16), in_spe...]
    unnamed x1, local copies, waits for them, and re-layouts: 6.31 us -> 2.88 us
where the time goes in v2:
time: 95.1 us; the launch traced here: 95 us
  Pallas kernels  92.1 us (97%)
  local copies, waits for them, and re-layouts  2.88 us (3%)
    pallas_call x1, Pallas kernels, step(): pl.pallas_call(kernel, out_shape=VMEM((count, d_model, ff), bf16), in_spe...  92.1 us
    unnamed x1, local copies, waits for them, and re-layouts  2.88 us

profile of v2, /device:TPU:96, one launch (start us, length us, event | category | flops | bytes accessed | tf_op | source)
XLA Modules:
  0.0 95.0 jit_solution(5017143626319765323)
XLA Ops:
  0.0 92.1 %sums.1 = bf16[4,512,1664]{2,1,0:T(8,128)(2,1)S(1)} custom-call(bf16[4,4096,512]{2,1,0:T(8,128)(2,1)} %bitcast.3, bf16[4,4096,1664]{2,1,0:T(8,128)(2,1)} %bitcast.2), custom_call_target="tpu_custom_call" | custom-call | tf_op jit(solution)/shard_map/sums/pallas_call | solution.py:236
  92.2 2.9 %copy.4 = bf16[4,512,1664]{2,1,0:T(8,128)(2,1)} copy(bf16[4,512,1664]{2,1,0:T(8,128)(2,1)S(1)} %sums.1) | data formatting | bytes 13631488

commit v3 on v2

v3 whole, which is shorter than its diff:
```python
import functools

import jax
import jax.numpy as jnp
from jax import lax
from jax.experimental import pallas as pl
from jax.experimental.pallas import tpu as pltpu
from jax.sharding import PartitionSpec as P

MESH = pl.DeviceIdType.MESH
SIDE = 4
LANES = 128
LAST = 7
TILES = (7, 6)
LAG = (0, 3, 6, 8, 10, 12, 16, 23)
FIRST = 4


def kernel(a_hbm, g_hbm, out, a_buf, g_buf, terms, s0, r1, s1, r2, rows, s2, r3, s3, r4,
           first_sem, a_sem, g_sem, send_sem, recv_sem, last_sem):
    count, tokens, d_model = a_hbm.shape
    columns = []
    for t in TILES:
        columns.append((sum(w for _, w in columns), t * LANES))
    per = len(columns)
    half_rows = d_model // 2
    block = half_rows // SIDE
    side_rows = block // 2
    sub = block // SIDE

    me = lax.axis_index("dp")
    px, py = me // SIDE, me % SIDE
    ring_x = [px] + [(px + i) % SIDE for i in (1, 2, 3)]
    ring_y = [py] + [(py + i) % SIDE for i in (1, 2, 3)]
    first, second = (ring_x, ring_y), (ring_y, ring_x)
    device_x = [p * SIDE + py for p in ring_x]
    device_y = [px * SIDE + p for p in ring_y]
    device_first, device_second = (device_x, device_y), (device_y, device_x)

    def of(h, i, k=None):
        row = h * half_rows + first[h][i % SIDE] * block
        return pl.multiple_of(row if k is None else row + k * sub, sub)

    def a_load(n, h):
        rows_of = pl.ds(h * half_rows, half_rows)
        return pltpu.make_async_copy(a_hbm.at[n, :, rows_of], a_buf.at[n % 2, :, rows_of], a_sem.at[n % 2, h])

    def g_load(n, j):
        c, w = columns[j]
        slot = (n * per + j) % 2
        return pltpu.make_async_copy(g_hbm.at[n, :, pl.ds(c, w)], g_buf.at[slot, :, pl.ds(0, w)], g_sem.at[slot])

    def first_loads(k):
        part = tokens // FIRST
        at, (c, w) = pl.ds(k * part, part), columns[0]
        rows_of = pl.ds(0, half_rows)
        return (pltpu.make_async_copy(a_hbm.at[0, at, rows_of], a_buf.at[0, at, rows_of], first_sem.at[0, k]),
                pltpu.make_async_copy(g_hbm.at[0, at, pl.ds(c, w)], g_buf.at[0, at, pl.ds(0, w)], first_sem.at[1, k]))

    for k in range(FIRST):
        for load in first_loads(k):
            load.start()
    a_load(0, 1).start()
    g_load(0, 1).start()
    a_load(1, 0).start()

    barrier = pltpu.get_barrier_semaphore()
    for i in (1, 3):
        pl.semaphore_signal(barrier, inc=1, device_id={"dp": device_x[i]}, device_id_type=MESH)
        pl.semaphore_signal(barrier, inc=1, device_id={"dp": device_y[i]}, device_id_type=MESH)

    for k in range(FIRST):
        for load in first_loads(k):
            load.wait()
        part, (c, w) = tokens // FIRST, columns[0]
        at = pl.ds(k * part, part)
        term = lax.dot_general(
            a_buf[0, at, pl.ds(0, half_rows)], g_buf[0, at, pl.ds(0, w)],
            (((0,), (0,)), ((), ())), preferred_element_type=jnp.float32)
        if k:
            term += terms[0, pl.ds(0, half_rows), pl.ds(c, w)]
        terms[0, pl.ds(0, half_rows), pl.ds(c, w)] = term

    pl.semaphore_wait(barrier, SIDE)

    def matmul(n, j, h):
        c, w = columns[j]
        if j == 0:
            a_load(n, h).wait()

            @pl.when(n + 1 < count)
            def _():
                a_load(n + 1, h).start()
        if h == 0:
            g_load(n, j).wait()
            if j + 1 < per:
                g_load(n, j + 1).start()
            else:
                @pl.when(n + 1 < count)
                def _():
                    g_load(n + 1, 0).start()
        mine = pl.ds(h * half_rows, half_rows)
        terms[n, mine, pl.ds(c, w)] = lax.dot_general(
            a_buf[n % 2, :, mine], g_buf[(n * per + j) % 2, :, pl.ds(0, w)],
            (((0,), (0,)), ((), ())), preferred_element_type=jnp.float32)

    def stages(n, j, h):
        c, w = columns[j]
        cols = pl.ds(c, w)
        unit = n * per + j

        def term(row, size):
            return terms[n, pl.ds(row, size), cols]

        def send(src, dst, kind, device):
            pltpu.make_async_remote_copy(
                src_ref=src, dst_ref=dst, send_sem=send_sem.at[n],
                recv_sem=last_sem.at[n] if kind == LAST else recv_sem.at[kind, 2 * unit + h],
                device_id={"dp": device}, device_id_type=MESH).start()

        def arrived(kind, size):
            ref = out.at[n, pl.ds(0, size), cols]
            pltpu.make_async_copy(ref, ref, recv_sem.at[kind, 2 * unit + h]).wait()

        p, q = first[h], second[h]
        up, down = device_first[h][1], device_first[h][3]
        odd = (unit + h) % 2
        ahead, behind = q[1] + odd * (q[3] - q[1]), q[3] + odd * (q[1] - q[3])
        to = device_second[h]
        to_ahead, to_behind = to[1] + odd * (to[3] - to[1]), to[3] + odd * (to[1] - to[3])

        def at(buf, i, size):
            return buf.at[n, h, pl.ds(i * size, size), cols]

        def place(row, size):
            return out.at[n, pl.ds(row, size), cols]

        def mine(i):
            return rows[n, h, pl.ds(pl.multiple_of(i * sub, sub), sub), cols]

        half = side_rows

        def stage0():
            s0[n, h, pl.ds(0, block), cols] = term(of(h, 2), block).astype(jnp.bfloat16)
            s0[n, h, pl.ds(2 * half, half), cols] = term(of(h, 3) + half, half).astype(jnp.bfloat16)
            s0[n, h, pl.ds(3 * half, half), cols] = term(of(h, 1), half).astype(jnp.bfloat16)
            send(at(s0, 0, half), at(r1, 0, half), 0, down)
            send(at(s0, 1, half), at(r1, 1, half), 0, up)
            send(at(s0, 2, half), at(r2, 3, half), 1, down)
            send(at(s0, 3, half), at(r2, 2, half), 1, up)

        def stage1():
            arrived(0, 2 * half)
            got = r1[n, h, :, cols].astype(jnp.float32)
            s1[n, h, pl.ds(0, half), cols] = (got[:half] + term(of(h, 3), half)).astype(jnp.bfloat16)
            s1[n, h, pl.ds(half, half), cols] = (got[half:] + term(of(h, 1) + half, half)).astype(jnp.bfloat16)
            send(at(s1, 0, half), at(r2, 0, half), 1, down)
            send(at(s1, 1, half), at(r2, 1, half), 1, up)

        def stage2():
            arrived(1, 4 * half)
            got = r2[n, h, :, cols].astype(jnp.float32)
            rows[n, h, :, cols] = got[:block] + got[block:] + term(of(h, 0), block)
            s2[n, h, pl.ds(0, sub), cols] = mine(q[2]).astype(jnp.bfloat16)
            s2[n, h, pl.ds(sub, sub), cols] = mine(ahead).astype(jnp.bfloat16)
            send(at(s2, 0, sub), at(r3, 0, sub), 2, to_behind)
            send(at(s2, 1, sub), at(r4, 1, sub), 3, to_ahead)

        def stage3():
            arrived(2, sub)
            s3[n, h, :, cols] = (r3[n, h, :, cols].astype(jnp.float32) + mine(behind)).astype(jnp.bfloat16)
            send(at(s3, 0, sub), at(r4, 0, sub), 3, to_behind)

        def stage4():
            arrived(3, 2 * sub)
            got = r4[n, h, :, cols].astype(jnp.float32)
            row = of(h, 0, q[0])
            out[n, pl.ds(row, sub), cols] = (got[:sub] + got[sub:] + mine(q[0])).astype(jnp.bfloat16)
            for i in (1, 3):
                send(place(row, sub), place(row, sub), 4, to[i])

        def stage5():
            arrived(4, 2 * sub)
            row = of(h, 0, behind)
            send(place(row, sub), place(row, sub), 5, to_ahead)

        def stage6():
            arrived(5, sub)
            row = of(h, 0)
            send(place(row, block), place(row, block), 6, up)
            send(place(row, block), place(row, block), 6, down)

        def stage7():
            arrived(6, 2 * block)
            row = of(h, 3)
            send(place(row, half), place(row, half), LAST, up)
            row = of(h, 1) + half
            send(place(row, half), place(row, half), LAST, down)

        return stage0, stage1, stage2, stage3, stage4, stage5, stage6, stage7

    def step(it, _):
        for tick in range(2 * per):
            @pl.when(it < count)
            def _():
                stages(it, tick // 2, tick % 2)[0]()

            for s in range(len(LAG) - 1, 0, -1):
                back = -((tick - LAG[s]) // (2 * per))
                then = (tick - LAG[s]) % (2 * per)
                n = it - back

                @pl.when((n >= 0) & (n < count))
                def _():
                    stages(n, then // 2, then % 2)[s]()

            later = (tick + 1) % (2 * per)
            n = it if later else it + 1

            @pl.when(n < count)
            def _():
                matmul(n, later // 2, later % 2)
        return 0

    lax.fori_loop(0, count + -(-LAG[-1] // (2 * per)), step, 0)

    def finish(n, _):
        ref = out.at[pl.ds(0, 2), pl.ds(0, 15 * half_rows // 8)]
        pltpu.make_async_copy(ref, ref, send_sem.at[n]).wait()
        ref = out.at[0, pl.ds(0, 4 * side_rows)]
        pltpu.make_async_copy(ref, ref, last_sem.at[n]).wait()
        return 0

    lax.fori_loop(0, count, finish, 0)


def solution(mesh):
    def step(a, g):
        a, g = a.reshape(a.shape[1:]), g.reshape(g.shape[1:])
        count, tokens, d_model = a.shape
        ff = g.shape[2]
        assert mesh.shape["dp"] == SIDE * SIDE and sum(TILES) * LANES == ff
        units = count * len(TILES)
        bf16, f32 = jnp.bfloat16, jnp.float32
        half_rows = d_model // 2
        block = half_rows // SIDE
        sub = block // SIDE
        VMEM, DMA = pltpu.VMEM, pltpu.SemaphoreType.DMA
        return pl.pallas_call(
            kernel,
            out_shape=VMEM((count, d_model, ff), bf16),
            in_specs=[pl.BlockSpec(memory_space=pl.ANY)] * 2,
            out_specs=pl.BlockSpec(memory_space=VMEM),
            scratch_shapes=[
                VMEM((2, tokens, d_model), bf16),
                VMEM((2, tokens, max(TILES) * LANES), bf16),
                VMEM((count, d_model, ff), f32),
                VMEM((count, 2, 2 * block, ff), bf16),
                VMEM((count, 2, block, ff), bf16),
                VMEM((count, 2, block, ff), bf16),
                VMEM((count, 2, 2 * block, ff), bf16),
                VMEM((count, 2, block, ff), f32),
                VMEM((count, 2, 2 * sub, ff), bf16),
                VMEM((count, 2, sub, ff), bf16),
                VMEM((count, 2, sub, ff), bf16),
                VMEM((count, 2, 2 * sub, ff), bf16),
                DMA((2, FIRST)),
                DMA((2, 2)),
                DMA((2,)),
                DMA((count,)),
                DMA((LAST, 2 * units)),
                DMA((count,)),
            ],
            compiler_params=pltpu.CompilerParams(
                collective_id=0, has_side_effects=True, vmem_limit_bytes=57 * 1024 * 1024),
            name="sums",
        )(a, g)

    return jax.shard_map(
        step, mesh=mesh, in_specs=(P(("rep", "dp")), P(("rep", "dp"))), out_specs=P("rep"), check_vma=False)
```

time: 95.1 us -> 90.3 us (0.950)
  Pallas kernels: 92.1 us -> 86.8 us
    pallas_call x1, Pallas kernels: 92.1 us -> 86.8 us  [step(): pl.pallas_call(kernel, out_shape=VMEM((count, d_model, ff), bf16), in_spe...]
where the time goes in v3:
time: 90.3 us; the launch traced here: 89.7 us
  Pallas kernels  86.8 us (96%)
  local copies, waits for them, and re-layouts  2.88 us (3%)
    pallas_call x1, Pallas kernels, step(): pl.pallas_call(kernel, out_shape=VMEM((count, d_model, ff), bf16), in_spe...  86.8 us
    unnamed x1, local copies, waits for them, and re-layouts  2.88 us

profile of v3, /device:TPU:96, one launch (start us, length us, event | category | flops | bytes accessed | tf_op | source)
XLA Modules:
  0.0 89.7 jit_solution(166604306442837722)
XLA Ops:
  0.0 86.8 %sums.1 = bf16[4,512,1664]{2,1,0:T(8,128)(2,1)S(1)} custom-call(bf16[4,4096,512]{2,1,0:T(8,128)(2,1)} %bitcast.3, bf16[4,4096,1664]{2,1,0:T(8,128)(2,1)} %bitcast.2), custom_call_target="tpu_custom_call" | custom-call | tf_op jit(solution)/shard_map/sums/pallas_call | solution.py:249
  86.9 2.9 %copy.4 = bf16[4,512,1664]{2,1,0:T(8,128)(2,1)} copy(bf16[4,512,1664]{2,1,0:T(8,128)(2,1)S(1)} %sums.1) | data formatting | bytes 13631488

commit v4 on v3

--- a/solution.py
+++ b/solution.py
@@ -11,8 +11,10 @@
 SIDE = 4
 LANES = 128
 LAST = 7
+SHARED = (0, 1, 2, 3, 1, 2, 0)
 TILES = (7, 6)
 LAG = (0, 3, 6, 8, 10, 12, 16, 23)
+ORDER = (7, 6, 5, 4, 3, 2, 1)
 FIRST = 4
 
 
@@ -115,12 +117,12 @@
         def send(src, dst, kind, device):
             pltpu.make_async_remote_copy(
                 src_ref=src, dst_ref=dst, send_sem=send_sem.at[n],
-                recv_sem=last_sem.at[n] if kind == LAST else recv_sem.at[kind, 2 * unit + h],
+                recv_sem=last_sem.at[n] if kind == LAST else recv_sem.at[SHARED[kind], 2 * unit + h],
                 device_id={"dp": device}, device_id_type=MESH).start()
 
         def arrived(kind, size):
             ref = out.at[n, pl.ds(0, size), cols]
-            pltpu.make_async_copy(ref, ref, recv_sem.at[kind, 2 * unit + h]).wait()
+            pltpu.make_async_copy(ref, ref, recv_sem.at[SHARED[kind], 2 * unit + h]).wait()
 
         p, q = first[h], second[h]
         up, down = device_first[h][1], device_first[h][3]
@@ -205,7 +207,7 @@
             def _():
                 stages(it, tick // 2, tick % 2)[0]()
 
-            for s in range(len(LAG) - 1, 0, -1):
+            for s in ORDER:
                 back = -((tick - LAG[s]) // (2 * per))
                 then = (tick - LAG[s]) % (2 * per)
                 n = it - back
@@ -268,7 +270,7 @@
                 DMA((2, 2)),
                 DMA((2,)),
                 DMA((count,)),
-                DMA((LAST, 2 * units)),
+                DMA((max(SHARED) + 1, 2 * units)),
                 DMA((count,)),
             ],
             compiler_params=pltpu.CompilerParams(

time: 90.3 us -> 89.9 us (level)
  no operation moved by 1% of the time
where the time goes in v4:
time: 89.9 us; the launch traced here: 89.3 us
  Pallas kernels  86.4 us (96%)
  local copies, waits for them, and re-layouts  2.88 us (3%)
    pallas_call x1, Pallas kernels, step(): pl.pallas_call(kernel, out_shape=VMEM((count, d_model, ff), bf16), in_spe...  86.4 us
    unnamed x1, local copies, waits for them, and re-layouts  2.88 us

profile of v4, /device:TPU:96, one launch (start us, length us, event | category | flops | bytes accessed | tf_op | source)
XLA Modules:
  0.0 89.3 jit_solution(9944941318834222686)
XLA Ops:
  0.0 86.4 %sums.1 = bf16[4,512,1664]{2,1,0:T(8,128)(2,1)S(1)} custom-call(bf16[4,4096,512]{2,1,0:T(8,128)(2,1)} %bitcast.3, bf16[4,4096,1664]{2,1,0:T(8,128)(2,1)} %bitcast.2), custom_call_target="tpu_custom_call" | custom-call | tf_op jit(solution)/shard_map/sums/pallas_call | solution.py:251
  86.4 2.9 %copy.4 = bf16[4,512,1664]{2,1,0:T(8,128)(2,1)} copy(bf16[4,512,1664]{2,1,0:T(8,128)(2,1)S(1)} %sums.1) | data formatting | bytes 13631488

commit v5 on v4

--- a/solution.py
+++ b/solution.py
@@ -13,7 +13,7 @@
 LAST = 7
 SHARED = (0, 1, 2, 3, 1, 2, 0)
 TILES = (7, 6)
-LAG = (0, 3, 6, 8, 10, 12, 16, 23)
+LAG = (0, 3, 6, 8, 10, 12, 16, 25)
 ORDER = (7, 6, 5, 4, 3, 2, 1)
 FIRST = 4
 

time: 89.9 us -> 89.8 us (level)
  no operation moved by 1% of the time
where the time goes in v5:
time: 89.8 us; the launch traced here: 89.3 us
  Pallas kernels  86.4 us (96%)
  local copies, waits for them, and re-layouts  2.88 us (3%)
    pallas_call x1, Pallas kernels, step(): pl.pallas_call(kernel, out_shape=VMEM((count, d_model, ff), bf16), in_spe...  86.4 us
    unnamed x1, local copies, waits for them, and re-layouts  2.88 us

profile of v5, /device:TPU:96, one launch (start us, length us, event | category | flops | bytes accessed | tf_op | source)
XLA Modules:
  0.0 89.3 jit_solution(16111428273996319133)
XLA Ops:
  0.0 86.4 %sums.1 = bf16[4,512,1664]{2,1,0:T(8,128)(2,1)S(1)} custom-call(bf16[4,4096,512]{2,1,0:T(8,128)(2,1)} %bitcast.3, bf16[4,4096,1664]{2,1,0:T(8,128)(2,1)} %bitcast.2), custom_call_target="tpu_custom_call" | custom-call | tf_op jit(solution)/shard_map/sums/pallas_call | solution.py:251
  86.5 2.9 %copy.4 = bf16[4,512,1664]{2,1,0:T(8,128)(2,1)} copy(bf16[4,512,1664]{2,1,0:T(8,128)(2,1)S(1)} %sums.1) | data formatting | bytes 13631488
